TPU v7x, 32 devices: a whole 2x2x4 slice. The times are simulated.
32 devices in a mesh: grp: 4 (over y, x), sub: 8 (over z, core).
Axes of the slice: x: 2, y: 2, z: 4, core: 2. Of those that a mesh axis runs over, the one named last changes fastest.
Arguments:
- reg_disp: float32 [4, 8, 3, 384], P('grp', 'sub'), may hold values from -6 to 6
- reg_vel: float32 [4, 8, 3, 384], P('grp', 'sub'), may hold values from -0.6 to 0.6
- site_disp: float32 [4, 8, 3, 1536], P('grp', 'sub'), may hold values from -6 to 6
- site_vel: float32 [4, 8, 3, 1536], P('grp', 'sub'), may hold values from -0.6 to 0.6
- reg_nodes: int32 [4, 8, 10, 256], P('grp', 'sub'), may hold values from 0 to 383
- site_nodes: int32 [4, 8, 35, 128], P('grp', 'sub'), may hold values from 0 to 1535
- reg_coefs: float32 [4, 8, 3, 3, 4, 256], P('grp', 'sub'), may hold values from -1.5 to 6, as said below
- site_coefs: float32 [4, 8, 3, 3, 24, 128], P('grp', 'sub'), may hold values from -1.5 to 6, as said below
- reg_table: float32 [12, 10], replicated, may hold values from -2 to 2
- site_table: float32 [72, 35], replicated, may hold values from -1 to 1
- reg_minv: float32 [4, 8, 384], P('grp', 'sub'), may hold values from 0.003 to 0.015
- site_minv: float32 [4, 8, 1536], P('grp', 'sub'), may hold values from 0.003 to 0.015
- reg_send: int32 [4, 8, 2, 128], P('grp', 'sub'), may hold values from 0 to 383
- reg_recv: int32 [4, 8, 2, 128], P('grp', 'sub'), may hold values from 0 to 383
- site_send: int32 [4, 8, 2, 128], P('grp', 'sub'), may hold values from 0 to 1535
- site_recv: int32 [4, 8, 2, 128], P('grp', 'sub'), may hold values from 0 to 1535
- slot_fill: int32 [4, 8, 4], P('grp', 'sub'), may hold values from 1 to 128, 384 in all within a row
- layer_src: int32 [4, 8, 128], P('grp', 'sub'), may hold values from 0 to 383
- layer_fill: int32 [4, 8], P('grp', 'sub'), may hold values from 64 to 128, as said below
- layer_dst: int32 [4, 8, 3, 128], P('grp', 'sub'), may hold values from 0 to 1535
- layer_stiff: float32 [4, 8, 3, 128], P('grp', 'sub'), may hold values from 0.5 to 2
Outputs:
- reg_final: float32 [4, 8, 3, 384], P('grp', 'sub')
- site_final: float32 [4, 8, 3, 1536], P('grp', 'sub')
Inputs may be any that keep to these rules, and one draw needn't show every extreme that they name: `slot_fill`: per partition the four entries count live slots toward the lower and higher neighbour, regional then site; they sum to 384. `layer_fill`: partition index 0 of every group fills all 128 slots. `reg_coefs`: each 3 x 3 tensor over the first two dimensions is symmetric positive definite. `site_coefs`: each 3 x 3 tensor over the first two dimensions is symmetric positive definite.
All inputs are finite; a program needn't handle non-finite values.
Results may differ from a plain program's by a relative error of at most 0.0003.
Values sent between devices are 32-bit elements; how exact they have to be, the bound alone decides.
A program may use at most 64 MiB of HBM per device.

v0:
```python
import functools

import jax
import jax.numpy as jnp
from jax import lax
from jax.experimental import pallas as pl
from jax.experimental.pallas import tpu as pltpu
from jax.sharding import PartitionSpec as P

STEPS = 8
LANES = 128
MESH = pl.DeviceIdType.MESH
F32 = jnp.float32
BF16 = jnp.bfloat16


def up(size, unit):
    return -(-size // unit) * unit


def lane_gather(block, index):
    numbers = lax.GatherDimensionNumbers(
        offset_dims=(),
        collapsed_slice_dims=(1,),
        start_index_map=(1,),
        operand_batching_dims=(0,),
        start_indices_batching_dims=(0,),
    )
    return lax.gather(
        block,
        index[..., None],
        numbers,
        slice_sizes=(1, 1),
        mode=lax.GatherScatterMode.PROMISE_IN_BOUNDS,
    )


def split(value):
    high = value.astype(BF16)
    low = (value - high.astype(F32)).astype(BF16)
    return high, low


def dot(left, right):
    return jnp.dot(left, right, preferred_element_type=F32)


def spread(rows, blocks, row_block):
    lanes = rows[0].shape[1]
    mine = lax.broadcasted_iota(jnp.int32, (row_block, lanes), 0) == blocks
    return jnp.concatenate([jnp.where(mine, row, 0.0) for row in rows], axis=0).astype(BF16)


def spread_block(block, blocks, row_block):
    high = block.astype(BF16).astype(F32)
    low = block - high
    rows = [part[c : c + 1] for part in (high, low) for c in range(3)]
    return spread(rows, blocks, row_block)


def fill_onehot(out_ref, first_row, lanes_index, tmp_ref):
    count, length = len(lanes_index), lanes_index[0].shape[1]
    tmp_ref[...] = jnp.zeros_like(tmp_ref)
    for r, row in enumerate(lanes_index):
        tmp_ref[r : r + 1, :] = row.astype(F32)
    columns = tmp_ref[...].T
    lane = lax.broadcasted_iota(jnp.int32, (length, LANES), 1).astype(F32)
    for r in range(count):
        hot = jnp.where(lane == columns[:, r : r + 1], 1.0, 0.0)
        out_ref[first_row + r * length : first_row + (r + 1) * length, :] = hot.astype(BF16)


def pick(field, lanes_index, blocks, row_block):
    slots = lanes_index.shape[1]
    index = jnp.broadcast_to(lanes_index, (row_block, slots))
    mine = lax.broadcasted_iota(jnp.int32, (row_block, slots), 0) == blocks
    out = []
    for c in range(3):
        got = lane_gather(field[c * row_block : (c + 1) * row_block], index)
        out.append(jnp.sum(jnp.where(mine, got, 0.0), axis=0, keepdims=True))
    return out


def sizes(nodes_shape, coefs_shape, disp_shape):
    p, _, e = nodes_shape
    q = coefs_shape[-2]
    h = disp_shape[-1] // LANES
    qp = up(q, 8)
    return dict(p=p, e=e, q=q, h=h, hp=up(h, 8), qp=qp, p8=up(p, 8), pp=up(p, 16), kp=up(3 * qp, 16))


def role_scratch(d, extra_rows):
    return [
        pltpu.VMEM((d["p8"], d["e"]), jnp.int32),
        pltpu.VMEM((d["p8"], d["e"]), jnp.int32),
        pltpu.VMEM((d["p"] * d["e"], LANES), BF16),
        pltpu.VMEM((extra_rows * LANES, LANES), BF16),
        pltpu.VMEM((6 * d["hp"], d["p"] * d["e"]), BF16),
        pltpu.VMEM((2, d["pp"], 3 * d["e"]), F32),
        pltpu.VMEM((9, d["qp"], d["e"]), F32),
        pltpu.VMEM((2 * d["kp"], d["pp"]), BF16),
        pltpu.VMEM((2 * d["pp"], d["kp"]), BF16),
        pltpu.VMEM((3 * d["hp"], LANES), F32),
        pltpu.VMEM((3 * d["hp"], LANES), F32),
        pltpu.VMEM((3 * d["hp"], LANES), F32),
        pltpu.VMEM((LANES, d["e"]), F32),
    ]


def prepare(d, s, disp, vel, nodes, coefs, table, minv, slot_rows, square, tmp):
    (lane_ref, block_ref, hot_ref, slot_hot_ref, _, _, coef_ref, dd_ref, dt_ref, u_ref, prev_ref, minv_ref, tp) = s
    p, q, qp, kp, pp, hp = d["p"], d["q"], d["qp"], d["kp"], d["pp"], d["hp"]
    lane_ref[...] = jnp.zeros_like(lane_ref)
    block_ref[...] = jnp.full_like(block_ref, -1)
    for r in range(p):
        lane_ref[r : r + 1, :] = nodes[r] & (LANES - 1)
        block_ref[r : r + 1, :] = nodes[r] >> 7
    fill_onehot(hot_ref, 0, [nodes[r] & (LANES - 1) for r in range(p)], tp)
    fill_onehot(slot_hot_ref, 0, [row & (LANES - 1) for row in slot_rows], tmp)
    if qp != q:
        coef_ref[...] = jnp.zeros_like(coef_ref)
    coef_ref[:, 0:q, :] = coefs[...]
    square[...] = jnp.zeros_like(square)
    turned_table = table.shape[0] == p
    for b in range(3):
        if turned_table:
            square[0:p, b * qp : b * qp + q] = table[:, b * q : (b + 1) * q]
        else:
            square[b * qp : b * qp + q, 0:p] = table[b * q : (b + 1) * q, :]

    def plain():
        high, low = split(square[0:kp, 0:pp])
        dd_ref[0:kp, :] = high
        dd_ref[kp : 2 * kp, :] = low

    def turned():
        high, low = split(-square[0:pp, 0:kp])
        dt_ref[0:pp, :] = high
        dt_ref[pp : 2 * pp, :] = low

    first, second = (turned, plain) if turned_table else (plain, turned)
    first()
    square[...] = square[...].T
    second()
    for ref in (u_ref, prev_ref, minv_ref):
        ref[...] = jnp.zeros_like(ref)
    for c in range(3):
        for h in range(d["h"]):
            at, cut = c * hp + h, slice(h * LANES, (h + 1) * LANES)
            now = disp[c, :, cut]
            u_ref[at : at + 1, :] = now
            prev_ref[at : at + 1, :] = now - vel[c, :, cut]
            minv_ref[at : at + 1, :] = minv[0, :, cut]


def element_forces(d, s):
    (lane_ref, block_ref, hot_ref, _, left_ref, fe_ref, coef_ref, dd_ref, dt_ref, u_ref, _, _, _) = s
    p, e, qp, kp, pp, p8, hp = d["p"], d["e"], d["qp"], d["kp"], d["pp"], d["p8"], d["hp"]
    tiles = e // LANES
    got = [[jnp.zeros((p8, LANES), F32) for _ in range(tiles)] for _ in range(3)]
    for t in range(tiles):
        cut = slice(t * LANES, (t + 1) * LANES)
        lanes_index, blocks = lane_ref[:, cut], block_ref[:, cut]
        for h in range(d["h"]):
            mine = blocks == h
            for c in range(3):
                row = jnp.broadcast_to(u_ref[c * hp + h : c * hp + h + 1, :], (p8, LANES))
                got[c][t] = jnp.where(mine, lane_gather(row, lanes_index), got[c][t])
    nodal = jnp.concatenate([got[c][t] for c in range(3) for t in range(tiles)], axis=1)
    if pp != p8:
        nodal = jnp.concatenate([nodal, jnp.zeros((pp - p8, 3 * e), F32)], axis=0)
    high, low = split(nodal)
    both = dot(dd_ref[...], high)
    grad = both[0:kp] + both[kp:] + dot(dd_ref[0:kp, :], low)
    fluxes = []
    for c in range(3):
        cut = slice(c * e, (c + 1) * e)
        pieces = [grad[b * qp : (b + 1) * qp, cut] for b in range(3)]
        rows = [
            coef_ref[3 * a] * pieces[0] + coef_ref[3 * a + 1] * pieces[1] + coef_ref[3 * a + 2] * pieces[2]
            for a in range(3)
        ]
        if kp != 3 * qp:
            rows.append(jnp.zeros((kp - 3 * qp, e), F32))
        fluxes.append(jnp.concatenate(rows, axis=0))
    high, low = split(jnp.concatenate(fluxes, axis=1))
    both = dot(dt_ref[...], high)
    force = both[0:pp] + both[pp:] + dot(dt_ref[0:pp, :], low)
    high = force.astype(BF16).astype(F32)
    fe_ref[0] = high
    fe_ref[1] = force - high
    for n in range(p):
        rows = [fe_ref[k, n : n + 1, c * e : (c + 1) * e] for k in range(2) for c in range(3)]
        left_ref[:, n * e : (n + 1) * e] = spread(rows, block_ref[n : n + 1, :], hp)
    total = dot(left_ref[...], hot_ref[...])
    return total[0 : 3 * hp] + total[3 * hp :]


def kernel(
    n_grp, n_sub, rd, sd,
    reg_disp, reg_vel, site_disp, site_vel, reg_nodes, site_nodes, reg_coefs, site_coefs,
    reg_table, site_table, reg_minv, site_minv, reg_send, reg_recv, site_send, site_recv,
    slot_fill, layer_src, layer_fill, layer_dst, layer_stiff,
    reg_out, site_out,
    send_ref, recv_ref, layer_send_ref, layer_recv_ref, square, tmp,
    halo_send, halo_recv, layer_send, layer_recv,
    *scratch,
):
    half = len(scratch) // 2
    rs, ss = scratch[:half], scratch[half:]
    slots = reg_send.shape[1]
    sites = n_grp // 4
    regs = 3 * sites
    grp, sub = lax.axis_index("grp"), lax.axis_index("sub")
    is_site = grp >= regs
    has_low, has_high = sub > 0, sub < n_sub - 1
    source, part = grp // sites, grp % sites

    barrier = pltpu.get_barrier_semaphore()

    def greet(target):
        pl.semaphore_signal(barrier, inc=1, device_id=target, device_id_type=MESH)

    @pl.when(has_low)
    def _():
        greet((grp, sub - 1))

    @pl.when(has_high)
    def _():
        greet((grp, sub + 1))

    @pl.when(is_site)
    def _():
        for m in range(3):
            greet((m * sites + part, sub))

    def meet(others):
        peers = jnp.minimum(sub, 1) + jnp.minimum(n_sub - 1 - sub, 1) + others
        pl.semaphore_wait(barrier, peers)

    def halo(n, side):
        target = sub - 1 if side == 0 else sub + 1
        return pltpu.make_async_remote_copy(
            src_ref=send_ref.at[n, side],
            dst_ref=recv_ref.at[n, 1 - side],
            send_sem=halo_send.at[n, side],
            recv_sem=halo_recv.at[n, 1 - side],
            device_id=(grp, target),
            device_id_type=MESH,
        )

    def arrival(n, side):
        target = sub - 1 if side == 0 else sub + 1
        return pltpu.make_async_remote_copy(
            src_ref=send_ref.at[n, side],
            dst_ref=recv_ref.at[n, side],
            send_sem=halo_send.at[n, side],
            recv_sem=halo_recv.at[n, side],
            device_id=(grp, target),
            device_id_type=MESH,
        )

    def layer_copy(n, m):
        return pltpu.make_async_remote_copy(
            src_ref=layer_send_ref.at[n],
            dst_ref=layer_recv_ref.at[n, m],
            send_sem=layer_send.at[n],
            recv_sem=layer_recv.at[n, m],
            device_id=(regs + part, sub),
            device_id_type=MESH,
        )

    send_ref[...] = jnp.zeros_like(send_ref)

    @pl.when(jnp.logical_not(has_low))
    def _():
        recv_ref[:, 0] = jnp.zeros((STEPS, 8, slots), F32)

    @pl.when(jnp.logical_not(has_high))
    def _():
        recv_ref[:, 1] = jnp.zeros((STEPS, 8, slots), F32)

    lane = lax.broadcasted_iota(jnp.int32, (1, slots), 1)

    def exchange_start(n, force, send_map, first_fill, hp):
        for side in range(2):
            fill = slot_fill[0, :, first_fill + side : first_fill + side + 1]
            index = send_map[side : side + 1, :]
            blocks = jnp.where(lane < fill, index >> 7, -1)
            rows = pick(force, index & (LANES - 1), blocks, hp)
            for c in range(3):
                send_ref[n, side, c : c + 1, :] = rows[c]

        @pl.when(has_low)
        def _():
            halo(n, 0).start()

        @pl.when(has_high)
        def _():
            halo(n, 1).start()

    def exchange_end(n, recv_map, hot, hp):
        @pl.when(has_low)
        def _():
            arrival(n, 0).wait_recv()

        @pl.when(has_high)
        def _():
            arrival(n, 1).wait_recv()

        left = [
            spread_block(recv_ref[n, side], recv_map[side : side + 1, :] >> 7, hp) for side in range(2)
        ]
        total = dot(jnp.concatenate(left, axis=1), hot)
        return total[0 : 3 * hp] + total[3 * hp :]

    def step_on(s, force):
        u_ref, prev_ref, minv_ref = s[9], s[10], s[11]
        now = u_ref[...]
        later = 2.0 * now - prev_ref[...] + minv_ref[...] * force
        prev_ref[...] = now
        u_ref[...] = later
        return later

    def finish(d, s, out):
        for c in range(3):
            for h in range(d["h"]):
                at = c * d["hp"] + h
                out[c, :, h * LANES : (h + 1) * LANES] = s[9][at : at + 1, :]

    def drain():
        def body(n, carry):
            @pl.when(has_low)
            def _():
                halo(n, 0).wait_send()

            @pl.when(has_high)
            def _():
                halo(n, 1).wait_send()

            return carry

        lax.fori_loop(0, STEPS, body, 0)

    @pl.when(jnp.logical_not(is_site))
    def _():
        site_out[...] = jnp.zeros_like(site_out)
        layer_send_ref[...] = jnp.zeros_like(layer_send_ref)
        prepare(rd, rs, reg_disp, reg_vel, reg_nodes, reg_coefs, reg_table, reg_minv, [reg_recv[k : k + 1, :] for k in range(2)], square, tmp)
        meet(1)
        hp = rd["hp"]

        def body(n, carry):
            force = element_forces(rd, rs)
            exchange_start(n, force, reg_send, 0, hp)
            force = force + exchange_end(n, reg_recv, rs[3][...], hp)
            later = step_on(rs, force)
            index = layer_src[0]
            blocks = jnp.where(lane < layer_fill[...], index >> 7, -1)
            rows = pick(later, index & (LANES - 1), blocks, hp)
            for c in range(3):
                layer_send_ref[n, c : c + 1, :] = rows[c]
            layer_copy(n, source).start()
            return carry

        lax.fori_loop(0, STEPS, body, 0)
        finish(rd, rs, reg_out)
        drain()

        def last(n, carry):
            layer_copy(n, source).wait_send()
            return carry

        lax.fori_loop(0, STEPS, last, 0)

    @pl.when(is_site)
    def _():
        reg_out[...] = jnp.zeros_like(reg_out)
        prepare(
            sd, ss, site_disp, site_vel, site_nodes, site_coefs, site_table, site_minv,
            [site_recv[k : k + 1, :] for k in range(2)] + [layer_dst[m] for m in range(3)], square, tmp,
        )
        meet(0)
        hp = sd["hp"]

        def body(n, carry):
            force = element_forces(sd, ss)
            exchange_start(n, force, site_send, 2, hp)
            for m in range(3):
                layer_copy(n, m).wait_recv()
            left = [
                spread_block(
                    layer_recv_ref[n, m] * layer_stiff[m], layer_dst[m] >> 7, hp
                )
                for m in range(3)
            ]
            total = dot(jnp.concatenate(left, axis=1), ss[3][2 * slots :, :])
            force = force + total[0 : 3 * hp] + total[3 * hp :]
            force = force + exchange_end(n, site_recv, ss[3][0 : 2 * slots, :], hp)
            step_on(ss, force)
            return carry

        lax.fori_loop(0, STEPS, body, 0)
        finish(sd, ss, site_out)
        drain()


def solution(mesh):
    n_grp, n_sub = mesh.shape["grp"], mesh.shape["sub"]

    def shards(*args):
        args = list(args)
        for k in (0, 1, 2, 3, 4, 5, 19, 20):
            rows, length = args[k].shape[2:]
            args[k] = jnp.transpose(args[k], (0, 2, 1, 3)).reshape(rows, 1, length)
        for k in (12, 13, 14, 15):
            args[k] = args[k].reshape(args[k].shape[2:])
        args[9] = args[9].T
        for k in (6, 7):
            args[k] = args[k].reshape((9,) + args[k].shape[4:])
        rd = sizes(args[4].shape, args[6].shape, args[0].shape)
        sd = sizes(args[5].shape, args[7].shape, args[2].shape)
        slots = args[12].shape[1]
        vmem = pl.BlockSpec(memory_space=pltpu.VMEM)
        reg_out, site_out = pl.pallas_call(
            functools.partial(kernel, n_grp, n_sub, rd, sd),
            out_shape=(
                jax.ShapeDtypeStruct(args[0].shape, F32),
                jax.ShapeDtypeStruct(args[2].shape, F32),
            ),
            in_specs=[vmem] * len(args),
            out_specs=(vmem, vmem),
            scratch_shapes=[
                pltpu.VMEM((STEPS, 2, 8, slots), F32),
                pltpu.VMEM((STEPS, 2, 8, slots), F32),
                pltpu.VMEM((STEPS, 8, slots), F32),
                pltpu.VMEM((STEPS, 3, 8, slots), F32),
                pltpu.VMEM((LANES, LANES), F32),
                pltpu.VMEM((LANES, slots), F32),
                pltpu.SemaphoreType.DMA((STEPS, 2)),
                pltpu.SemaphoreType.DMA((STEPS, 2)),
                pltpu.SemaphoreType.DMA((STEPS,)),
                pltpu.SemaphoreType.DMA((STEPS, 3)),
            ]
            + role_scratch(rd, 2)
            + role_scratch(sd, 5),
            compiler_params=pltpu.CompilerParams(
                collective_id=0, has_side_effects=True
            ),
        )(*args)
        return tuple(out.reshape(1, 1, out.shape[0], out.shape[2]) for out in (reg_out, site_out))

    cell = ("grp", "sub")
    specs = [P(*cell)] * 21
    specs[8] = specs[9] = P()
    return jax.shard_map(
        shards,
        mesh=mesh,
        in_specs=tuple(specs),
        out_specs=(P(*cell), P(*cell)),
        check_vma=False,
    )
```

profile of v0, /device:TPU:7, one launch (start us, length us, event | category | flops | bytes accessed | tf_op | source)
XLA Modules:
  0.0 39.7 jit_solution(9977000801379480816)
XLA Ops:
  1.3 35.8 %shard_map.212 = (f32[3,1,384]{2,1,0:T(1,128)}, f32[3,1,1536]{2,1,0:T(1,128)}) custom-call(f32[3,1,384]{2,1,0:T(1,128)} %bitcast.30, f32[3,1,384]{2,1,0:T(1,128)} %bitcast.31, f32[3,1,1536]{2,1,0:T(1,128)} %bitcast.24, f32[3,1,1536]{2,1,0:T(1,128)} %bitcast.25, s32[10,1,256]{2,1,0:T(1,128)} %bitcast.28, s32[35,1,128]{2,1,0:T(1,128)} %bitcast.27, ...), custom_call_target="tpu_custom_call" | custom-call | tf_op jit(solution)/shard_map/pallas_call | solution.py:425
  37.1 0.0 copy-start
  37.1 0.7 %copy-done = f32[3,1,384]{2,1,0:T(1,128)S(1)} copy-done((f32[3,1,384]{2,1,0:T(1,128)S(1)}, f32[3,1,384]{2,1,0:T(1,128)}, u32[]{:S(2)}) %copy-start) | copy-done | bytes 4632
  37.8 0.6 %copy.28 = f32[1,1,3,384]{3,1,2,0:T(1,128)} copy(f32[1,1,3,384]{3,1,2,0:T(1,128)S(1)} %bitcast.29) | data formatting | bytes 9216
  38.4 1.3 %copy.29 = f32[1,1,3,1536]{3,1,2,0:T(1,128)} copy(f32[1,1,3,1536]{3,1,2,0:T(1,128)} %bitcast.26) | data formatting | bytes 36864
Async XLA Ops:
  37.1 0.7 %copy-start = (f32[3,1,384]{2,1,0:T(1,128)S(1)}, f32[3,1,384]{2,1,0:T(1,128)}, u32[]{:S(2)}) copy-start(f32[3,1,384]{2,1,0:T(1,128)} %get-tuple-element.4) | copy-start | bytes 13828
where the time goes:
time: 40.3 us; the launch traced here: 39.7 us
  Pallas kernels  35.8 us (89%)
  local copies, waits for them, and re-layouts  2.6 us (6%)
  between operations  1.3 us (3%)
    pallas_call x1, Pallas kernels, shards(): pl.pallas_call(functools.partial(kernel, n_grp, n_sub, rd, sd), out_shape...  35.8 us
    unnamed x4, local copies, waits for them, and re-layouts  2.6 us

commit v1 on v0

v1 whole, which is shorter than its diff:
```python
import functools

import jax
import jax.numpy as jnp
from jax import lax
from jax.experimental import pallas as pl
from jax.experimental.pallas import tpu as pltpu
from jax.sharding import PartitionSpec as P

STEPS = 8
LANES = 128
MESH = pl.DeviceIdType.MESH
F32 = jnp.float32
BF16 = jnp.bfloat16


def up(size, unit):
    return -(-size // unit) * unit


def lane_gather(block, index):
    numbers = lax.GatherDimensionNumbers(
        offset_dims=(),
        collapsed_slice_dims=(1,),
        start_index_map=(1,),
        operand_batching_dims=(0,),
        start_indices_batching_dims=(0,),
    )
    return lax.gather(
        block,
        index[..., None],
        numbers,
        slice_sizes=(1, 1),
        mode=lax.GatherScatterMode.PROMISE_IN_BOUNDS,
    )


def split(value):
    high = value.astype(BF16)
    low = (value - high.astype(F32)).astype(BF16)
    return high, low


def dot(left, right):
    return jnp.dot(left, right, preferred_element_type=F32)


def sizes(nodes_shape, coefs_shape, disp_shape):
    p, _, e = nodes_shape
    q = coefs_shape[-2]
    count = disp_shape[-1]
    width = LANES
    h = -(-count // width)
    qp = up(q, 8)
    return dict(
        p=p, e=e, q=q, count=count, width=width, shift=width.bit_length() - 1, h=h, hp=up(h, 8), qp=qp,
        p8=up(p, 8), pp=up(p, 16), kp=up(3 * qp, 16),
    )


def role_scratch(d, slot_rows, slots):
    return dict(
        lane=pltpu.VMEM((d["p8"], d["e"]), jnp.int32),
        block=pltpu.VMEM((d["p8"], d["e"]), jnp.int32),
        hot=pltpu.VMEM((d["p"] * d["e"], d["width"]), BF16),
        slot_hot=pltpu.VMEM((slot_rows * slots, d["width"]), BF16),
        fe=pltpu.VMEM((2, d["pp"], 3 * d["e"]), F32),
        coef=pltpu.VMEM((9, d["qp"], d["e"]), F32),
        dd=pltpu.VMEM((d["kp"], 3 * d["pp"]), BF16),
        dt=pltpu.VMEM((d["pp"], 3 * d["kp"]), BF16),
        u=pltpu.VMEM((3 * d["hp"], d["width"]), F32),
        prev=pltpu.VMEM((3 * d["hp"], d["width"]), F32),
        minv=pltpu.VMEM((3 * d["hp"], d["width"]), F32),
        turn=pltpu.VMEM((LANES, max(d["e"], slots)), F32),
    )


def fill_onehot(d, out_ref, rows, turn):
    length = rows[0].shape[1]
    for r, row in enumerate(rows):
        turn[r : r + 1, 0:length] = (row & (d["width"] - 1)).astype(F32)
    columns = turn[:, 0:length].T
    lane = lax.broadcasted_iota(jnp.int32, (length, d["width"]), 1).astype(F32)
    for r in range(len(rows)):
        hot = jnp.where(lane == columns[:, r : r + 1], 1.0, 0.0)
        out_ref[r * length : (r + 1) * length, :] = hot.astype(BF16)


def fill_tables(d, s, table, square):
    p, q, qp, kp, pp = d["p"], d["q"], d["qp"], d["kp"], d["pp"]
    square[...] = jnp.zeros_like(square)
    turned = table.shape[0] == p
    for b in range(3):
        if turned:
            square[0:p, b * qp : b * qp + q] = table[:, b * q : (b + 1) * q]
        else:
            square[b * qp : b * qp + q, 0:p] = table[b * q : (b + 1) * q, :]

    def plain():
        high, low = split(square[0:kp, 0:pp])
        s["dd"][...] = jnp.concatenate([high.astype(F32), low.astype(F32), high.astype(F32)], axis=1).astype(BF16)

    def flipped():
        high, low = split(-square[0:pp, 0:kp])
        s["dt"][...] = jnp.concatenate([high.astype(F32), low.astype(F32), high.astype(F32)], axis=1).astype(BF16)

    first, second = (flipped, plain) if turned else (plain, flipped)
    first()
    square[...] = square[...].T
    second()


def fill_nodes(d, s, nodes, slot_rows):
    p = d["p"]
    s["lane"][...] = jnp.zeros_like(s["lane"])
    s["block"][...] = jnp.full_like(s["block"], -1)
    for r in range(p):
        s["lane"][r : r + 1, :] = nodes[r] & (LANES - 1)
        s["block"][r : r + 1, :] = nodes[r] >> 7
    s["turn"][...] = jnp.zeros_like(s["turn"])
    fill_onehot(d, s["hot"], [nodes[r] for r in range(p)], s["turn"])
    fill_onehot(d, s["slot_hot"], slot_rows, s["turn"])


def fill_state(d, s, disp, vel, minv):
    hp, width, count = d["hp"], d["width"], d["count"]
    for ref in (s["u"], s["prev"], s["minv"]):
        ref[...] = jnp.zeros_like(ref)
    for c in range(3):
        for h in range(d["h"]):
            size = min(width, count - h * width)
            at, cut = c * hp + h, slice(h * width, h * width + size)
            now = disp[c, :, cut]
            s["u"][at : at + 1, 0:size] = now
            s["prev"][at : at + 1, 0:size] = now - vel[c, :, cut]
            s["minv"][at : at + 1, 0:size] = minv[0, :, cut]


def fill_coefs(d, s, coefs):
    if d["qp"] != d["q"]:
        s["coef"][...] = jnp.zeros_like(s["coef"])
    s["coef"][:, 0 : d["q"], :] = coefs[...]


def spread(d, rows, blocks):
    lanes = rows[0].shape[1]
    mine = lax.broadcasted_iota(jnp.int32, (d["hp"], lanes), 0) == blocks
    return jnp.concatenate([jnp.where(mine, row, 0.0) for row in rows], axis=0).astype(BF16)


def spread_block(d, block, index):
    high = block.astype(BF16).astype(F32)
    low = block - high
    rows = [part[c : c + 1] for part in (high, low) for c in range(3)]
    return spread(d, rows, index >> d["shift"])


def join(d, total):
    half = 3 * d["hp"]
    return total[0:half] + total[half:]


def pick(d, field, index, live):
    hp, slots = d["hp"], index.shape[1]
    lane = jnp.broadcast_to(index & (LANES - 1), (hp, slots))
    blocks = jnp.where(live, index >> d["shift"], -1)
    mine = lax.broadcasted_iota(jnp.int32, (hp, slots), 0) == blocks
    parts = d["width"] // LANES
    which = jnp.broadcast_to((index >> 7) & (parts - 1), (hp, slots))
    out = []
    for c in range(3):
        rows = field[c * hp : (c + 1) * hp]
        got = lane_gather(rows[:, 0:LANES], lane)
        for k in range(1, parts):
            got = jnp.where(which == k, lane_gather(rows[:, k * LANES : (k + 1) * LANES], lane), got)
        out.append(jnp.sum(jnp.where(mine, got, 0.0), axis=0, keepdims=True))
    return out


def element_forces(d, s):
    p, e, qp, kp, pp, p8, hp = d["p"], d["e"], d["qp"], d["kp"], d["pp"], d["p8"], d["hp"]
    parts = d["width"] // LANES
    blocks128 = -(-d["count"] // LANES)
    tiles = e // LANES
    groups = p8 // 8
    got = {}
    for t in range(tiles):
        cut = slice(t * LANES, (t + 1) * LANES)
        for g in range(groups):
            lane = s["lane"][8 * g : 8 * g + 8, cut]
            block = s["block"][8 * g : 8 * g + 8, cut]
            bits = [(block >> k) & 1 == 1 for k in range((blocks128 - 1).bit_length())]
            for c in range(3):
                values = []
                for h in range(blocks128):
                    at, part = h // parts, h % parts
                    row = s["u"][c * hp + at : c * hp + at + 1, part * LANES : (part + 1) * LANES]
                    values.append(lane_gather(jnp.broadcast_to(row, (8, LANES)), lane))
                for bit in bits:
                    values = [
                        jnp.where(bit, values[k + 1], values[k]) if k + 1 < len(values) else values[k]
                        for k in range(0, len(values), 2)
                    ]
                got[c, t, g] = values[0]
    rows = [
        jnp.concatenate([got[c, t, g] for c in range(3) for t in range(tiles)], axis=1) for g in range(groups)
    ]
    if pp != p8:
        rows.append(jnp.zeros((pp - p8, 3 * e), F32))
    high, low = split(jnp.concatenate(rows, axis=0))
    grad = dot(s["dd"][...], jnp.concatenate([high, high, low], axis=0))
    fluxes = []
    for c in range(3):
        cut = slice(c * e, (c + 1) * e)
        pieces = [grad[b * qp : (b + 1) * qp, cut] for b in range(3)]
        rows = [
            s["coef"][3 * a] * pieces[0] + s["coef"][3 * a + 1] * pieces[1] + s["coef"][3 * a + 2] * pieces[2]
            for a in range(3)
        ]
        if kp != 3 * qp:
            rows.append(jnp.zeros((kp - 3 * qp, e), F32))
        fluxes.append(jnp.concatenate(rows, axis=0))
    high, low = split(jnp.concatenate(fluxes, axis=1))
    force = dot(s["dt"][...], jnp.concatenate([high, high, low], axis=0))
    high = force.astype(BF16).astype(F32)
    s["fe"][0] = high
    s["fe"][1] = force - high
    up_shift = parts.bit_length() - 1
    step = max(1, 2 * LANES // e)
    total = None
    for first in range(0, p, step):
        chunk = range(first, min(p, first + step))
        left = []
        for n in chunk:
            rows = [s["fe"][k, n : n + 1, c * e : (c + 1) * e] for k in range(2) for c in range(3)]
            left.append(spread(d, rows, s["block"][n : n + 1, :] >> up_shift))
        piece = dot(jnp.concatenate(left, axis=1), s["hot"][first * e : (chunk[-1] + 1) * e, :])
        total = piece if total is None else total + piece
    return join(d, total)


SCALAR = 18
REG_INPUTS = (0, 1, 4, 6, 8, 10, 12, 13, 16, 17)
SITE_INPUTS = (2, 3, 5, 7, 9, 11, 14, 15, 16, 19, 20)
NAMES = ("disp", "vel", "nodes", "coefs", "table", "minv", "send", "recv", "fill", "x", "y")


def kernel(n_grp, n_sub, rd, sd, slots, *refs):
    inputs, (reg_out, site_out), refs = refs[:21], refs[21:23], refs[23:]
    (send_ref, recv_ref, layer_send_ref, layer_recv_ref, square, halo_send, halo_recv, layer_send, layer_recv, load_sem), refs = refs[:10], refs[10:]
    layer_fill = inputs[SCALAR]
    keys = list(role_scratch(rd, 2, slots))
    rs, refs = dict(zip(keys, refs)), refs[len(keys) :]
    ss, refs = dict(zip(keys, refs)), refs[len(keys) :]
    count = len(REG_INPUTS)
    reg_in, site_in = refs[:count], refs[count:]
    sites = n_grp // 4
    regs = 3 * sites
    grp, sub = lax.axis_index("grp"), lax.axis_index("sub")
    is_site = grp >= regs
    has_low, has_high = sub > 0, sub < n_sub - 1
    source, part = grp // sites, grp % sites

    def loads(numbers, places):
        return {
            name: pltpu.make_async_copy(inputs[k], place, load_sem.at[i])
            for i, (name, k, place) in enumerate(zip(NAMES, numbers, places))
        }

    reg_loads, site_loads = loads(REG_INPUTS, reg_in), loads(SITE_INPUTS, site_in)
    first = ("nodes", "recv", "x", "table", "coefs", "disp", "vel", "minv", "send", "fill", "y")

    @pl.when(jnp.logical_not(is_site))
    def _():
        for name in first[:-1]:
            reg_loads[name].start()

    @pl.when(is_site)
    def _():
        for name in first:
            site_loads[name].start()

    barrier = pltpu.get_barrier_semaphore()

    def greet(target):
        pl.semaphore_signal(barrier, inc=1, device_id=target, device_id_type=MESH)

    @pl.when(has_low)
    def _():
        greet((grp, sub - 1))

    @pl.when(has_high)
    def _():
        greet((grp, sub + 1))

    @pl.when(is_site)
    def _():
        for m in range(3):
            greet((m * sites + part, sub))

    def meet(others):
        peers = jnp.minimum(sub, 1) + jnp.minimum(n_sub - 1 - sub, 1) + others
        pl.semaphore_wait(barrier, peers)

    def halo(n, side):
        target = sub - 1 if side == 0 else sub + 1
        return pltpu.make_async_remote_copy(
            src_ref=send_ref.at[n, side],
            dst_ref=recv_ref.at[n, 1 - side],
            send_sem=halo_send.at[n, side],
            recv_sem=halo_recv.at[n, 1 - side],
            device_id=(grp, target),
            device_id_type=MESH,
        )

    def arrival(n, side):
        target = sub - 1 if side == 0 else sub + 1
        return pltpu.make_async_remote_copy(
            src_ref=send_ref.at[n, side],
            dst_ref=recv_ref.at[n, side],
            send_sem=halo_send.at[n, side],
            recv_sem=halo_recv.at[n, side],
            device_id=(grp, target),
            device_id_type=MESH,
        )

    def layer_copy(n, m):
        return pltpu.make_async_remote_copy(
            src_ref=layer_send_ref.at[n],
            dst_ref=layer_recv_ref.at[n, m],
            send_sem=layer_send.at[n],
            recv_sem=layer_recv.at[n, m],
            device_id=(regs + part, sub),
            device_id_type=MESH,
        )

    send_ref[...] = jnp.zeros_like(send_ref)

    @pl.when(jnp.logical_not(has_low))
    def _():
        recv_ref[:, 0] = jnp.zeros((STEPS, 8, slots), F32)

    @pl.when(jnp.logical_not(has_high))
    def _():
        recv_ref[:, 1] = jnp.zeros((STEPS, 8, slots), F32)

    lane = lax.broadcasted_iota(jnp.int32, (1, slots), 1)

    def exchange_start(d, n, force, send_map, fills, first_fill):
        for side in range(2):
            fill = fills[0, :, first_fill + side : first_fill + side + 1]
            rows = pick(d, force, send_map[side : side + 1, :], lane < fill)
            for c in range(3):
                send_ref[n, side, c : c + 1, :] = rows[c]

        @pl.when(has_low)
        def _():
            halo(n, 0).start()

        @pl.when(has_high)
        def _():
            halo(n, 1).start()

    def exchange_end(d, n, recv_map, hot):
        @pl.when(has_low)
        def _():
            arrival(n, 0).wait_recv()

        @pl.when(has_high)
        def _():
            arrival(n, 1).wait_recv()

        left = [spread_block(d, recv_ref[n, side], recv_map[side : side + 1, :]) for side in range(2)]
        return join(d, dot(jnp.concatenate(left, axis=1), hot))

    def step_on(s, force):
        now = s["u"][...]
        later = 2.0 * now - s["prev"][...] + s["minv"][...] * force
        s["prev"][...] = now
        s["u"][...] = later
        return later

    def finish(d, s, out):
        width, total = d["width"], d["count"]
        for c in range(3):
            for h in range(d["h"]):
                at, size = c * d["hp"] + h, min(width, total - h * width)
                out[c, :, h * width : h * width + size] = s["u"][at : at + 1, 0:size]

    def drain():
        def body(n, carry):
            @pl.when(has_low)
            def _():
                halo(n, 0).wait_send()

            @pl.when(has_high)
            def _():
                halo(n, 1).wait_send()

            return carry

        lax.fori_loop(0, STEPS, body, 0)

    @pl.when(jnp.logical_not(is_site))
    def _():
        v = dict(zip(NAMES, reg_in))
        site_out[...] = jnp.zeros_like(site_out)
        layer_send_ref[...] = jnp.zeros_like(layer_send_ref)
        for name in ("nodes", "recv"):
            reg_loads[name].wait()
        fill_nodes(rd, rs, v["nodes"], [v["recv"][k : k + 1, :] for k in range(2)])
        for name in first[:-1]:
            if name not in ("nodes", "recv"):
                reg_loads[name].wait()
        fill_tables(rd, rs, v["table"], square)
        fill_coefs(rd, rs, v["coefs"])
        fill_state(rd, rs, v["disp"], v["vel"], v["minv"])
        meet(1)

        def body(n, carry):
            force = element_forces(rd, rs)
            exchange_start(rd, n, force, v["send"], v["fill"], 0)
            force = force + exchange_end(rd, n, v["recv"], rs["slot_hot"][...])
            later = step_on(rs, force)
            rows = pick(rd, later, v["x"][0], lane < layer_fill[...])
            for c in range(3):
                layer_send_ref[n, c : c + 1, :] = rows[c]
            layer_copy(n, source).start()
            return carry

        lax.fori_loop(0, STEPS, body, 0)
        finish(rd, rs, reg_out)
        drain()

        def last(n, carry):
            layer_copy(n, source).wait_send()
            return carry

        lax.fori_loop(0, STEPS, last, 0)

    @pl.when(is_site)
    def _():
        v = dict(zip(NAMES, site_in))
        reg_out[...] = jnp.zeros_like(reg_out)
        early = ("nodes", "recv", "x")
        for name in early:
            site_loads[name].wait()
        fill_nodes(sd, ss, v["nodes"], [v["recv"][k : k + 1, :] for k in range(2)] + [v["x"][m] for m in range(3)])
        for name in first:
            if name not in early:
                site_loads[name].wait()
        fill_tables(sd, ss, v["table"], square)
        fill_coefs(sd, ss, v["coefs"])
        fill_state(sd, ss, v["disp"], v["vel"], v["minv"])
        meet(0)

        def body(n, carry):
            force = element_forces(sd, ss)
            exchange_start(sd, n, force, v["send"], v["fill"], 2)
            for m in range(3):
                layer_copy(n, m).wait_recv()
            left = [spread_block(sd, layer_recv_ref[n, m] * v["y"][m], v["x"][m]) for m in range(3)]
            force = force + join(sd, dot(jnp.concatenate(left, axis=1), ss["slot_hot"][2 * slots :, :]))
            force = force + exchange_end(sd, n, v["recv"], ss["slot_hot"][0 : 2 * slots, :])
            step_on(ss, force)
            return carry

        lax.fori_loop(0, STEPS, body, 0)
        finish(sd, ss, site_out)
        drain()


def solution(mesh):
    n_grp, n_sub = mesh.shape["grp"], mesh.shape["sub"]

    def shards(*args):
        args = list(args)
        for k in (0, 1, 2, 3, 4, 5, 19, 20):
            rows, length = args[k].shape[2:]
            args[k] = jnp.transpose(args[k], (0, 2, 1, 3)).reshape(rows, 1, length)
        for k in (12, 13, 14, 15):
            args[k] = args[k].reshape(args[k].shape[2:])
        args[9] = args[9].T
        for k in (6, 7):
            args[k] = args[k].reshape((9,) + args[k].shape[4:])
        rd = sizes(args[4].shape, args[6].shape, args[0].shape)
        sd = sizes(args[5].shape, args[7].shape, args[2].shape)
        slots = args[12].shape[1]
        vmem = pl.BlockSpec(memory_space=pltpu.VMEM)
        hbm = pl.BlockSpec(memory_space=pltpu.HBM)
        places = [pltpu.VMEM(args[k].shape, args[k].dtype) for k in REG_INPUTS + SITE_INPUTS]
        reg_out, site_out = pl.pallas_call(
            functools.partial(kernel, n_grp, n_sub, rd, sd, slots),
            out_shape=(
                jax.ShapeDtypeStruct(args[0].shape, F32),
                jax.ShapeDtypeStruct(args[2].shape, F32),
            ),
            in_specs=[vmem if k == SCALAR else hbm for k in range(len(args))],
            out_specs=(vmem, vmem),
            scratch_shapes=[
                pltpu.VMEM((STEPS, 2, 8, slots), F32),
                pltpu.VMEM((STEPS, 2, 8, slots), F32),
                pltpu.VMEM((STEPS, 8, slots), F32),
                pltpu.VMEM((STEPS, 3, 8, slots), F32),
                pltpu.VMEM((LANES, LANES), F32),
                pltpu.SemaphoreType.DMA((STEPS, 2)),
                pltpu.SemaphoreType.DMA((STEPS, 2)),
                pltpu.SemaphoreType.DMA((STEPS,)),
                pltpu.SemaphoreType.DMA((STEPS, 3)),
                pltpu.SemaphoreType.DMA((len(SITE_INPUTS),)),
            ]
            + list(role_scratch(rd, 2, slots).values())
            + list(role_scratch(sd, 5, slots).values())
            + places,
            compiler_params=pltpu.CompilerParams(
                collective_id=0, has_side_effects=True, vmem_limit_bytes=32 * 1024 * 1024
            ),
        )(*[arg if k == SCALAR else pltpu.with_memory_space_constraint(arg, pltpu.HBM) for k, arg in enumerate(args)])
        return tuple(out.reshape(1, 1, out.shape[0], out.shape[2]) for out in (reg_out, site_out))

    cell = ("grp", "sub")
    specs = [P(*cell)] * 21
    specs[8] = specs[9] = P()
    return jax.shard_map(
        shards,
        mesh=mesh,
        in_specs=tuple(specs),
        out_specs=(P(*cell), P(*cell)),
        check_vma=False,
    )
```

time: 40.3 us -> 35.6 us (0.88)
  Pallas kernels: 35.8 us -> 32.7 us
  local copies, waits for them, and re-layouts: 2.6 us -> 1.2 us
    pallas_call x1, Pallas kernels: 35.8 us -> 32.7 us  [shards(): pl.pallas_call(functools.partial(kernel, n_grp, n_sub, rd, sd, slots), ou...]
    unnamed x4 -> x2, local copies, waits for them, and re-layouts: 2.6 us -> 1.2 us
where the time goes in v1:
time: 35.6 us; the launch traced here: 35.2 us
  Pallas kernels  32.7 us (92%)
  between operations  1.29 us (4%)
  local copies, waits for them, and re-layouts  1.2 us (3%)
    pallas_call x1, Pallas kernels, shards(): pl.pallas_call(functools.partial(kernel, n_grp, n_sub, rd, sd, slots), ou...  32.7 us
    unnamed x2, local copies, waits for them, and re-layouts  1.2 us

profile of v1, /device:TPU:7, one launch (start us, length us, event | category | flops | bytes accessed | tf_op | source)
XLA Modules:
  0.0 35.2 jit_solution(5759104584982491230)
XLA Ops:
  1.3 32.7 %shard_map.212 = (f32[3,1,384]{2,1,0:T(1,128)S(1)}, f32[3,1,1536]{2,1,0:T(1,128)S(1)}) custom-call(f32[3,1,384]{2,1,0:T(1,128)} %bitcast.30, f32[3,1,384]{2,1,0:T(1,128)} %bitcast.31, f32[3,1,1536]{2,1,0:T(1,128)} %bitcast.26, f32[3,1,1536]{2,1,0:T(1,128)} %bitcast.27, s32[10,1,256]{2,1,0:T(1,128)} %bitcast.29, s32[35,1,128]{2,1,0:T(1,128)} %bitcast.28, ...), custom_call_target="tpu_custom_call" | custom-call | tf_op jit(solution)/shard_map/pallas_call | solution.py:492
  34.0 0.6 %copy.28 = f32[1,1,3,384]{3,1,2,0:T(1,128)} copy(f32[1,1,3,384]{3,1,2,0:T(1,128)S(1)} %bitcast.22) | data formatting | bytes 9216
  34.5 0.6 %copy.29 = f32[1,1,3,1536]{3,1,2,0:T(1,128)} copy(f32[1,1,3,1536]{3,1,2,0:T(1,128)S(1)} %bitcast.21) | data formatting | bytes 36864

commit v2 on v1

v2 whole, which is shorter than its diff:
```python
import functools

import jax
import jax.numpy as jnp
from jax import lax
from jax.experimental import pallas as pl
from jax.experimental.pallas import tpu as pltpu
from jax.sharding import PartitionSpec as P

STEPS = 8
ROUNDS = STEPS // 2
LANES = 128
MESH = pl.DeviceIdType.MESH
F32 = jnp.float32
BF16 = jnp.bfloat16


def up(size, unit):
    return -(-size // unit) * unit


def lane_gather(block, index):
    numbers = lax.GatherDimensionNumbers(
        offset_dims=(),
        collapsed_slice_dims=(1,),
        start_index_map=(1,),
        operand_batching_dims=(0,),
        start_indices_batching_dims=(0,),
    )
    return lax.gather(
        block,
        index[..., None],
        numbers,
        slice_sizes=(1, 1),
        mode=lax.GatherScatterMode.PROMISE_IN_BOUNDS,
    )


def split(value):
    high = value.astype(BF16)
    low = (value - high.astype(F32)).astype(BF16)
    return high, low


def dot(left, right):
    return jnp.dot(left, right, preferred_element_type=F32)


def sizes(nodes_shape, coefs_shape, disp_shape):
    p, _, e = nodes_shape
    q = coefs_shape[-2]
    count = disp_shape[-1]
    width = LANES
    h = -(-count // width)
    qp = up(q, 8)
    return dict(
        p=p, e=e, q=q, count=count, width=width, shift=width.bit_length() - 1, h=h, hp=up(h, 8), qp=qp,
        p8=up(p, 8), kw=up(9 * qp, LANES),
    )


def part_scratch(d, slot_rows, slots):
    state = (3 * d["hp"], d["width"])
    return dict(
        lane=pltpu.VMEM((d["p8"], d["e"]), jnp.int32),
        block=pltpu.VMEM((d["p8"], d["e"]), jnp.int32),
        hot=pltpu.VMEM((d["p"] * d["e"], d["width"]), BF16),
        slot_hot=pltpu.VMEM((slot_rows * slots, d["width"]), BF16),
        fe=pltpu.VMEM((2, d["p8"], 3 * d["e"]), F32),
        ve=pltpu.VMEM((3, d["p8"], d["e"]), F32),
        matrix=pltpu.VMEM((d["p"] * d["p8"], d["e"]), F32),
        u=pltpu.VMEM(state, F32),
        minv=pltpu.VMEM(state, F32),
    )


def role_scratch(d, slots):
    state = (3 * d["hp"], d["width"])
    return dict(
        wide=pltpu.VMEM((2, d["p8"], d["kw"]), F32),
        weight=pltpu.VMEM((2, up(d["p"] * d["p8"], 16), d["kw"]), BF16),
        cube=pltpu.VMEM((9 * d["qp"], d["e"]), F32),
        turn=pltpu.VMEM((LANES, max(d["e"], slots)), F32),
        prev=pltpu.VMEM(state, F32),
        w_send=pltpu.VMEM((ROUNDS,) + state, F32),
        w_recv=pltpu.VMEM((ROUNDS,) + state, F32),
    )


def fill_onehot(d, out_ref, rows, turn):
    length = rows[0].shape[1]
    for r, row in enumerate(rows):
        turn[r : r + 1, 0:length] = (row & (d["width"] - 1)).astype(F32)
    columns = turn[:, 0:length].T
    lane = lax.broadcasted_iota(jnp.int32, (length, d["width"]), 1).astype(F32)
    for r in range(len(rows)):
        hot = jnp.where(lane == columns[:, r : r + 1], 1.0, 0.0)
        out_ref[r * length : (r + 1) * length, :] = hot.astype(BF16)


def fill_tables(d, s, table, square):
    p, q, qp, p8 = d["p"], d["q"], d["qp"], d["p8"]
    wide = s["wide"]
    wide[...] = jnp.zeros_like(wide)
    if table.shape[0] != p:
        square[...] = jnp.zeros_like(square)
        square[0 : 3 * q, 0:p] = table[...]
        square[...] = square[...].T
        table = square
    for a in range(3):
        for b in range(3):
            at = (3 * a + b) * qp
            wide[0, 0:p, at : at + q] = table[0:p, a * q : (a + 1) * q]
            wide[1, 0:p, at : at + q] = table[0:p, b * q : (b + 1) * q]
    left = -wide[0]
    for first in range(0, p, 2):
        rows = range(first, min(p, first + 2))
        high, low = split(jnp.concatenate([left * wide[1, n : n + 1, :] for n in rows], axis=0))
        cut = slice(first * p8, (rows[-1] + 1) * p8)
        s["weight"][0, cut, :] = high
        s["weight"][1, cut, :] = low


def fill_nodes(d, s, nodes, slot_rows):
    p = d["p"]
    s["lane"][...] = jnp.zeros_like(s["lane"])
    s["block"][...] = jnp.full_like(s["block"], -1)
    for r in range(p):
        s["lane"][r : r + 1, :] = nodes[r] & (LANES - 1)
        s["block"][r : r + 1, :] = nodes[r] >> 7
    s["turn"][...] = jnp.zeros_like(s["turn"])
    fill_onehot(d, s["hot"], [nodes[r] for r in range(p)], s["turn"])
    fill_onehot(d, s["slot_hot"], slot_rows, s["turn"])


def fill_state(d, pairs):
    hp, width, count = d["hp"], d["width"], d["count"]
    for ref, _ in pairs:
        ref[...] = jnp.zeros_like(ref)
    for c in range(3):
        for h in range(d["h"]):
            size = min(width, count - h * width)
            at, cut = c * hp + h, slice(h * width, h * width + size)
            for ref, value in pairs:
                ref[at : at + 1, 0:size] = value(c, cut)


def fill_matrix(d, s, coefs):
    q, qp, p, p8, e, depth = d["q"], d["qp"], d["p"], d["p8"], d["e"], 9 * d["qp"]
    if qp != q:
        s["cube"][...] = jnp.zeros_like(s["cube"])
    for k in range(9):
        s["cube"][k * qp : k * qp + q, :] = coefs[k]
    high, low = split(s["cube"][...])
    both = jnp.concatenate([high, low], axis=1)
    for first in range(0, p, 2):
        cut = slice(first * p8, min(p, first + 2) * p8)
        wide = dot(s["weight"][0, cut, 0:depth], both)
        s["matrix"][cut, :] = wide[:, 0:e] + wide[:, e:] + dot(s["weight"][1, cut, 0:depth], high)


def spread(d, rows, blocks):
    lanes = rows[0].shape[1]
    mine = lax.broadcasted_iota(jnp.int32, (d["hp"], lanes), 0) == blocks
    return jnp.concatenate([jnp.where(mine, row, 0.0) for row in rows], axis=0).astype(BF16)


def spread_block(d, block, index):
    high = block.astype(BF16).astype(F32)
    low = block - high
    rows = [part[c : c + 1] for part in (high, low) for c in range(3)]
    return spread(d, rows, index >> d["shift"])


def join(d, total):
    half = 3 * d["hp"]
    return total[0:half] + total[half:]


def pick(d, field, index, live):
    hp, slots = d["hp"], index.shape[1]
    lane = jnp.broadcast_to(index & (LANES - 1), (hp, slots))
    blocks = jnp.where(live, index >> d["shift"], -1)
    mine = lax.broadcasted_iota(jnp.int32, (hp, slots), 0) == blocks
    parts = d["width"] // LANES
    which = jnp.broadcast_to((index >> 7) & (parts - 1), (hp, slots))
    out = []
    for c in range(3):
        rows = field[c * hp : (c + 1) * hp]
        got = lane_gather(rows[:, 0:LANES], lane)
        for k in range(1, parts):
            got = jnp.where(which == k, lane_gather(rows[:, k * LANES : (k + 1) * LANES], lane), got)
        out.append(jnp.sum(jnp.where(mine, got, 0.0), axis=0, keepdims=True))
    return out


def element_forces(d, s):
    p, e, p8, hp = d["p"], d["e"], d["p8"], d["hp"]
    parts = d["width"] // LANES
    blocks128 = -(-d["count"] // LANES)
    groups = p8 // 8
    for t in range(e // LANES):
        cut = slice(t * LANES, (t + 1) * LANES)
        for g in range(groups):
            lane = s["lane"][8 * g : 8 * g + 8, cut]
            block = s["block"][8 * g : 8 * g + 8, cut]
            bits = [(block >> k) & 1 == 1 for k in range((blocks128 - 1).bit_length())]
            for c in range(3):
                values = []
                for h in range(blocks128):
                    at, part = h // parts, h % parts
                    row = s["u"][c * hp + at : c * hp + at + 1, part * LANES : (part + 1) * LANES]
                    values.append(lane_gather(jnp.broadcast_to(row, (8, LANES)), lane))
                for bit in bits:
                    values = [
                        jnp.where(bit, values[k + 1], values[k]) if k + 1 < len(values) else values[k]
                        for k in range(0, len(values), 2)
                    ]
                s["ve"][c, 8 * g : 8 * g + 8, cut] = values[0]
        total = [[None] * groups for _ in range(3)]
        for n in range(p):
            rows = [s["ve"][c, n : n + 1, cut] for c in range(3)]
            for g in range(groups):
                weight = s["matrix"][n * p8 + 8 * g : n * p8 + 8 * g + 8, cut]
                for c in range(3):
                    term = weight * rows[c]
                    total[c][g] = term if n == 0 else total[c][g] + term
        for g in range(groups):
            for c in range(3):
                high = total[c][g].astype(BF16).astype(F32)
                at = slice(c * e + t * LANES, c * e + (t + 1) * LANES)
                s["fe"][0, 8 * g : 8 * g + 8, at] = high
                s["fe"][1, 8 * g : 8 * g + 8, at] = total[c][g] - high
    up_shift = parts.bit_length() - 1
    step = max(1, 2 * LANES // e)
    total = None
    for first in range(0, p, step):
        chunk = range(first, min(p, first + step))
        left = []
        for n in chunk:
            rows = [s["fe"][k, n : n + 1, c * e : (c + 1) * e] for k in range(2) for c in range(3)]
            left.append(spread(d, rows, s["block"][n : n + 1, :] >> up_shift))
        piece = dot(jnp.concatenate(left, axis=1), s["hot"][first * e : (chunk[-1] + 1) * e, :])
        total = piece if total is None else total + piece
    return join(d, total)


SCALAR = 18
REG_INPUTS = (0, 1, 4, 6, 8, 10, 12, 13, 16, 17)
SITE_INPUTS = (2, 3, 5, 7, 9, 11, 14, 15, 16, 19, 20)
NAMES = ("disp", "vel", "nodes", "coefs", "table", "minv", "send", "recv", "fill", "spot", "stiff")
REG_SHARED = ("nodes", "recv", "send", "fill", "minv", "coefs")
SITE_SHARED = ("nodes", "recv", "spot", "send", "fill", "minv", "stiff", "coefs")


def kernel(n_grp, n_sub, rd, sd, slots, keys, *refs):
    inputs, (reg_out, site_out), refs = refs[:21], refs[21:23], refs[23:]
    layer_fill = inputs[SCALAR]
    box = {}
    for group, names in keys:
        box[group], refs = dict(zip(names, refs)), refs[len(names) :]
    b = box["common"]
    sites = n_grp // 4
    regs = 3 * sites
    grp, sub = lax.axis_index("grp"), lax.axis_index("sub")
    is_site = grp >= regs
    source, part = grp // sites, grp % sites
    odd = lax.rem(sub, 2)
    cross_side, mate_side = odd, 1 - odd
    way = 2 * odd - 1
    cross, mate, beyond, behind = sub + way, sub - way, sub + 2 * way, sub - 2 * way

    def exists(place):
        return jnp.logical_and(place >= 0, place < n_sub)

    has_cross, has_mate, has_beyond, has_behind = (exists(place) for place in (cross, mate, beyond, behind))

    def count(flag):
        return jnp.where(flag, 1, 0)

    def remote(src, dst, send_sem, recv_sem, target):
        return pltpu.make_async_remote_copy(
            src_ref=src, dst_ref=dst, send_sem=send_sem, recv_sem=recv_sem, device_id=target, device_id_type=MESH
        )

    def loads(numbers, places):
        return {
            name: pltpu.make_async_copy(inputs[k], places[name], b["load_sem"].at[i])
            for i, (name, k) in enumerate(zip(NAMES, numbers))
        }

    reg_loads, site_loads = loads(REG_INPUTS, box["reg_in"]), loads(SITE_INPUTS, box["site_in"])
    first = ("nodes", "recv", "spot", "table", "coefs", "disp", "vel", "minv", "send", "fill", "stiff")

    @pl.when(jnp.logical_not(is_site))
    def _():
        for name in first:
            if name in reg_loads:
                reg_loads[name].start()

    @pl.when(is_site)
    def _():
        for name in first:
            site_loads[name].start()

    barrier = pltpu.get_barrier_semaphore()

    def greet(target):
        pl.semaphore_signal(barrier, inc=1, device_id=target, device_id_type=MESH)

    for flag, place in ((has_cross, cross), (has_mate, mate), (has_beyond, beyond)):

        @pl.when(flag)
        def _():
            greet((grp, place))

    @pl.when(is_site)
    def _():
        for m in range(3):
            greet((m * sites + part, sub))

    @pl.when(jnp.logical_and(is_site, has_cross))
    def _():
        for m in range(3):
            greet((m * sites + part, cross))

    for name in ("cross_send", "mate_send", "layer_send"):
        b[name][...] = jnp.zeros_like(b[name])

    for flag, names in ((has_cross, ("cross_recv",)), (has_mate, ("mate_recv",)), (has_beyond, ("far_recv",))):

        @pl.when(jnp.logical_not(flag))
        def _():
            for name in names:
                b[name][...] = jnp.zeros_like(b[name])

    lane = lax.broadcasted_iota(jnp.int32, (1, slots), 1)

    def role(site):
        prefix = "site" if site else "reg"
        d = sd if site else rd
        v, gv = box[prefix + "_in"], box[prefix + "_ghost_in"]
        shared, own, ghost = box[prefix + "_shared"], dict(box[prefix + "_own"]), dict(box[prefix + "_ghost"])
        for s in (own, ghost):
            s.update(shared)
        load = site_loads if site else reg_loads
        names = SITE_SHARED if site else REG_SHARED
        first_fill = 2 if site else 0
        hp = d["hp"]

        def cross_copy(r):
            return remote(b["cross_send"].at[r], b["cross_recv"].at[r], b["cross_ss"].at[r], b["cross_rs"].at[r], (grp, cross))

        def w_copy(r):
            return remote(own["w_send"].at[r], own["w_recv"].at[r], b["w_ss"].at[r], b["w_rs"].at[r], (grp, cross))

        def mate_copy(n):
            return remote(b["mate_send"].at[n], b["mate_recv"].at[n], b["mate_ss"].at[n], b["mate_rs"].at[n], (grp, mate))

        def far_copy(r, target):
            return remote(b["mate_send"].at[2 * r], b["far_recv"].at[r], b["far_ss"].at[r], b["far_rs"].at[r], (grp, target))

        def share_copy(k):
            return remote(v[names[k]], gv[names[k]], b["share_ss"].at[k], b["share_rs"].at[k], (grp, cross))

        def layer_copy(n, m):
            return remote(
                b["layer_send"].at[n], b["layer_recv"].at[n, m], b["layer_ss"].at[n], b["layer_rs"].at[n, m],
                (regs + part, sub),
            )

        def layer_ghost(r, m):
            return remote(
                b["layer_send"].at[2 * r], b["layer_far"].at[r, m], b["layer_gs"].at[r], b["layer_gr"].at[r, m],
                (regs + part, cross),
            )

        def limit(fills, side):
            low, high = (fills[0, :, first_fill + k : first_fill + k + 1] for k in range(2))
            return jnp.where(side == 0, low, high)

        def row(ref, side):
            return ref[pl.ds(side, 1), :]

        def put(ref, n, rows):
            for c in range(3):
                ref[n, c : c + 1, :] = rows[c]

        def slot_terms(s, maps, blocks, hot):
            left = [spread_block(d, block, index) for block, index in zip(blocks, maps)]
            return join(d, dot(jnp.concatenate(left, axis=1), hot))

        def layer_terms(s, w, ref, n):
            maps = [w["spot"][m] for m in range(3)]
            return slot_terms(s, maps, [ref[n, m] * w["stiff"][m] for m in range(3)], s["slot_hot"][2 * slots :, :])

        def send_layer(n, field):
            put(b["layer_send"], n, pick(d, field, v["spot"][0], lane < layer_fill[...]))
            layer_copy(n, source).start()

        early = names[:3] if site else names[:2]
        for name in early:
            load[name].wait()

        def slot_rows(w, near, far):
            return [row(w["recv"], near), row(w["recv"], far)] + ([w["spot"][m] for m in range(3)] if site else [])

        fill_nodes(d, own, v["nodes"], slot_rows(v, cross_side, mate_side))
        for name in first:
            if name in load and name not in early:
                load[name].wait()

        @pl.when(jnp.logical_not(has_cross))
        def _():
            for name in names:
                gv[name][...] = jnp.zeros_like(gv[name])
            own["w_recv"][...] = jnp.zeros_like(own["w_recv"])
            if site:
                b["layer_far"][...] = jnp.zeros_like(b["layer_far"])

        others = 0 if site else 1 + count(has_cross)
        pl.semaphore_wait(barrier, count(has_cross) + count(has_mate) + count(has_behind) + others)

        @pl.when(has_cross)
        def _():
            for k in range(len(names)):
                share_copy(k).start()

        fill_tables(d, own, v["table"], b["square"])
        fill_matrix(d, own, v["coefs"])
        fill_state(
            d,
            [
                (own["u"], lambda c, cut: v["disp"][c, :, cut]),
                (own["prev"], lambda c, cut: v["disp"][c, :, cut] - v["vel"][c, :, cut]),
                (own["minv"], lambda c, cut: v["minv"][0, :, cut]),
            ],
        )
        near_live = lane < limit(v["fill"], cross_side)
        mate_live = lane < limit(v["fill"], mate_side)

        def ghost_setup():
            @pl.when(has_cross)
            def _():
                for k in range(len(names)):
                    share_copy(k).wait_recv()

            fill_nodes(d, ghost, gv["nodes"], slot_rows(gv, mate_side, cross_side))
            fill_matrix(d, ghost, gv["coefs"])
            fill_state(d, [(ghost["minv"], lambda c, cut: gv["minv"][0, :, cut])])

        def body(r, carry):
            n = 2 * r
            force = element_forces(d, own)
            put(b["cross_send"], r, pick(d, force, row(v["send"], cross_side), near_live))

            @pl.when(has_cross)
            def _():
                cross_copy(r).start()

            put(b["mate_send"], n, pick(d, force, row(v["send"], mate_side), mate_live))

            @pl.when(has_mate)
            def _():
                mate_copy(n).start()

            @pl.when(has_behind)
            def _():
                far_copy(r, behind).start()

            now = own["u"][...]
            ahead = 2.0 * now - own["prev"][...] + own["minv"][...] * force
            own["w_send"][r] = ahead

            @pl.when(has_cross)
            def _():
                w_copy(r).start()

            pl.when(r == 0)(ghost_setup)

            extra = jnp.zeros_like(force)
            if site:
                for m in range(3):
                    layer_copy(n, m).wait_recv()
                extra = layer_terms(own, v, b["layer_recv"], n)

            @pl.when(has_mate)
            def _():
                mate_copy(n).wait_recv()

            @pl.when(has_cross)
            def _():
                cross_copy(r).wait_recv()

            maps = [row(v["recv"], cross_side), row(v["recv"], mate_side)]
            hot = own["slot_hot"][0 : 2 * slots, :]
            extra = extra + slot_terms(own, maps, [b["cross_recv"][r], b["mate_recv"][n]], hot)
            middle = ahead + own["minv"][...] * extra
            own["prev"][...] = now
            own["u"][...] = middle
            if not site:
                send_layer(n, middle)

                @pl.when(has_cross)
                def _():
                    layer_ghost(r, source).start()

            force = element_forces(d, own)
            put(b["mate_send"], n + 1, pick(d, force, row(v["send"], mate_side), mate_live))

            @pl.when(has_mate)
            def _():
                mate_copy(n + 1).start()

            extra = jnp.zeros_like(force)
            if site:

                @pl.when(has_cross)
                def _():
                    for m in range(3):
                        layer_ghost(r, m).wait_recv()

                extra = layer_terms(ghost, gv, b["layer_far"], r)

            @pl.when(has_beyond)
            def _():
                far_copy(r, beyond).wait_recv()

            @pl.when(has_cross)
            def _():
                w_copy(r).wait_recv()

            ghost_maps = [row(gv["recv"], mate_side), row(gv["recv"], cross_side)]
            hot = ghost["slot_hot"][0 : 2 * slots, :]
            extra = extra + slot_terms(ghost, ghost_maps, [b["cross_send"][r], b["far_recv"][r]], hot)
            ghost["u"][...] = own["w_recv"][r] + ghost["minv"][...] * extra
            ghost_force = element_forces(d, ghost)
            ghost_live = lane < limit(gv["fill"], mate_side)
            near = jnp.concatenate(pick(d, ghost_force, row(gv["send"], mate_side), ghost_live), axis=0)

            extra = force
            if site:
                for m in range(3):
                    layer_copy(n + 1, m).wait_recv()
                extra = extra + layer_terms(own, v, b["layer_recv"], n + 1)

            @pl.when(has_mate)
            def _():
                mate_copy(n + 1).wait_recv()

            hot = own["slot_hot"][0 : 2 * slots, :]
            extra = extra + slot_terms(own, maps, [near, b["mate_recv"][n + 1]], hot)
            later = 2.0 * middle - now + own["minv"][...] * extra
            own["prev"][...] = middle
            own["u"][...] = later
            if not site:
                send_layer(n + 1, later)
            return carry

        lax.fori_loop(0, ROUNDS, body, 0)
        out = site_out if site else reg_out
        for c in range(3):
            for h in range(d["h"]):
                at, size = c * hp + h, min(d["width"], d["count"] - h * d["width"])
                out[c, :, h * d["width"] : h * d["width"] + size] = own["u"][at : at + 1, 0:size]

        def drain(r, carry):
            @pl.when(has_cross)
            def _():
                cross_copy(r).wait_send()
                w_copy(r).wait_send()

            @pl.when(has_behind)
            def _():
                far_copy(r, behind).wait_send()

            for n in (2 * r, 2 * r + 1):

                @pl.when(has_mate)
                def _():
                    mate_copy(n).wait_send()

                if not site:
                    layer_copy(n, source).wait_send()

            if not site:

                @pl.when(has_cross)
                def _():
                    layer_ghost(r, source).wait_send()

            return carry

        lax.fori_loop(0, ROUNDS, drain, 0)

        @pl.when(has_cross)
        def _():
            for k in range(len(names)):
                share_copy(k).wait_send()

    @pl.when(jnp.logical_not(is_site))
    def _():
        site_out[...] = jnp.zeros_like(site_out)
        role(False)

    @pl.when(is_site)
    def _():
        reg_out[...] = jnp.zeros_like(reg_out)
        role(True)


def solution(mesh):
    n_grp, n_sub = mesh.shape["grp"], mesh.shape["sub"]

    def shards(*args):
        args = list(args)
        for k in (0, 1, 2, 3, 4, 5, 19, 20):
            rows, length = args[k].shape[2:]
            args[k] = jnp.transpose(args[k], (0, 2, 1, 3)).reshape(rows, 1, length)
        for k in (12, 13, 14, 15):
            args[k] = args[k].reshape(args[k].shape[2:])
        args[9] = args[9].T
        for k in (6, 7):
            args[k] = args[k].reshape((9,) + args[k].shape[4:])
        rd = sizes(args[4].shape, args[6].shape, args[0].shape)
        sd = sizes(args[5].shape, args[7].shape, args[2].shape)
        slots = args[12].shape[1]
        vmem = pl.BlockSpec(memory_space=pltpu.VMEM)
        hbm = pl.BlockSpec(memory_space=pltpu.HBM)
        dma = pltpu.SemaphoreType.DMA
        block = (8, slots)
        groups = {
            "common": dict(
                square=pltpu.VMEM((LANES, LANES), F32),
                cross_send=pltpu.VMEM((ROUNDS,) + block, F32),
                cross_recv=pltpu.VMEM((ROUNDS,) + block, F32),
                mate_send=pltpu.VMEM((STEPS,) + block, F32),
                mate_recv=pltpu.VMEM((STEPS,) + block, F32),
                far_recv=pltpu.VMEM((ROUNDS,) + block, F32),
                layer_send=pltpu.VMEM((STEPS,) + block, F32),
                layer_recv=pltpu.VMEM((STEPS, 3) + block, F32),
                layer_far=pltpu.VMEM((ROUNDS, 3) + block, F32),
                load_sem=dma((len(SITE_INPUTS),)),
                cross_ss=dma((ROUNDS,)),
                cross_rs=dma((ROUNDS,)),
                w_ss=dma((ROUNDS,)),
                w_rs=dma((ROUNDS,)),
                mate_ss=dma((STEPS,)),
                mate_rs=dma((STEPS,)),
                far_ss=dma((ROUNDS,)),
                far_rs=dma((ROUNDS,)),
                layer_ss=dma((STEPS,)),
                layer_rs=dma((STEPS, 3)),
                layer_gs=dma((ROUNDS,)),
                layer_gr=dma((ROUNDS, 3)),
                share_ss=dma((len(SITE_SHARED),)),
                share_rs=dma((len(SITE_SHARED),)),
            )
        }
        for prefix, d, numbers, shared, slot_rows in (
            ("reg", rd, REG_INPUTS, REG_SHARED, 2),
            ("site", sd, SITE_INPUTS, SITE_SHARED, 5),
        ):
            places = {name: pltpu.VMEM(args[k].shape, args[k].dtype) for name, k in zip(NAMES, numbers)}
            groups[prefix + "_in"] = places
            groups[prefix + "_ghost_in"] = {name: places[name] for name in shared}
            groups[prefix + "_shared"] = role_scratch(d, slots)
            groups[prefix + "_own"] = part_scratch(d, slot_rows, slots)
            groups[prefix + "_ghost"] = part_scratch(d, slot_rows, slots)
        keys = [(group, list(items)) for group, items in groups.items()]
        reg_out, site_out = pl.pallas_call(
            functools.partial(kernel, n_grp, n_sub, rd, sd, slots, keys),
            out_shape=(
                jax.ShapeDtypeStruct(args[0].shape, F32),
                jax.ShapeDtypeStruct(args[2].shape, F32),
            ),
            in_specs=[vmem if k == SCALAR else hbm for k in range(len(args))],
            out_specs=(vmem, vmem),
            scratch_shapes=[place for items in groups.values() for place in items.values()],
            compiler_params=pltpu.CompilerParams(
                collective_id=0, has_side_effects=True, vmem_limit_bytes=32 * 1024 * 1024
            ),
        )(*[arg if k == SCALAR else pltpu.with_memory_space_constraint(arg, pltpu.HBM) for k, arg in enumerate(args)])
        return tuple(out.reshape(1, 1, out.shape[0], out.shape[2]) for out in (reg_out, site_out))

    cell = ("grp", "sub")
    specs = [P(*cell)] * 21
    specs[8] = specs[9] = P()
    return jax.shard_map(
        shards,
        mesh=mesh,
        in_specs=tuple(specs),
        out_specs=(P(*cell), P(*cell)),
        check_vma=False,
    )
```

time: 35.6 us -> 32.5 us (0.913)
  Pallas kernels: 32.7 us -> 29.7 us
    pallas_call x1, Pallas kernels: 32.7 us -> 29.7 us  [shards(): pl.pallas_call(functools.partial(kernel, n_grp, n_sub, rd, sd, slots, key...]
where the time goes in v2:
time: 32.5 us; the launch traced here: 32.2 us
  Pallas kernels  29.7 us (91%)
  between operations  1.29 us (4%)
  local copies, waits for them, and re-layouts  1.2 us (4%)
    pallas_call x1, Pallas kernels, shards(): pl.pallas_call(functools.partial(kernel, n_grp, n_sub, rd, sd, slots, key...  29.7 us
    unnamed x2, local copies, waits for them, and re-layouts  1.2 us

profile of v2, /device:TPU:7, one launch (start us, length us, event | category | flops | bytes accessed | tf_op | source)
XLA Modules:
  0.0 32.2 jit_solution(15952845783344062488)
XLA Ops:
  1.3 29.7 %shard_map.212 = (f32[3,1,384]{2,1,0:T(1,128)S(1)}, f32[3,1,1536]{2,1,0:T(1,128)S(1)}) custom-call(f32[3,1,384]{2,1,0:T(1,128)} %bitcast.30, f32[3,1,384]{2,1,0:T(1,128)} %bitcast.31, f32[3,1,1536]{2,1,0:T(1,128)} %bitcast.26, f32[3,1,1536]{2,1,0:T(1,128)} %bitcast.27, s32[10,1,256]{2,1,0:T(1,128)} %bitcast.29, s32[35,1,128]{2,1,0:T(1,128)} %bitcast.28, ...), custom_call_target="tpu_custom_call" | custom-call | tf_op jit(solution)/shard_map/pallas_call | solution.py:671
  31.0 0.6 %copy.28 = f32[1,1,3,384]{3,1,2,0:T(1,128)} copy(f32[1,1,3,384]{3,1,2,0:T(1,128)S(1)} %bitcast.22) | data formatting | bytes 9216
  31.6 0.6 %copy.29 = f32[1,1,3,1536]{3,1,2,0:T(1,128)} copy(f32[1,1,3,1536]{3,1,2,0:T(1,128)S(1)} %bitcast.21) | data formatting | bytes 36864

commit v3 on v2

--- a/solution.py
+++ b/solution.py
@@ -82,6 +82,7 @@
         cube=pltpu.VMEM((9 * d["qp"], d["e"]), F32),
         turn=pltpu.VMEM((LANES, max(d["e"], slots)), F32),
         prev=pltpu.VMEM(state, F32),
+        force=pltpu.VMEM(state, F32),
         w_send=pltpu.VMEM((ROUNDS,) + state, F32),
         w_recv=pltpu.VMEM((ROUNDS,) + state, F32),
     )
@@ -418,14 +419,17 @@
             if site:
                 b["layer_far"][...] = jnp.zeros_like(b["layer_far"])
 
-        others = 0 if site else 1 + count(has_cross)
-        pl.semaphore_wait(barrier, count(has_cross) + count(has_mate) + count(has_behind) + others)
-
-        @pl.when(has_cross)
-        def _():
-            for k in range(len(names)):
-                share_copy(k).start()
-
+        def meet_and_share():
+            others = 0 if site else 1 + count(has_cross)
+            pl.semaphore_wait(barrier, count(has_cross) + count(has_mate) + count(has_behind) + others)
+
+            @pl.when(has_cross)
+            def _():
+                for k in range(len(names)):
+                    share_copy(k).start()
+
+        if site:
+            meet_and_share()
         fill_tables(d, own, v["table"], b["square"])
         fill_matrix(d, own, v["coefs"])
         fill_state(
@@ -451,7 +455,7 @@
 
         def body(r, carry):
             n = 2 * r
-            force = element_forces(d, own)
+            force = own["force"][...]
             put(b["cross_send"], r, pick(d, force, row(v["send"], cross_side), near_live))
 
             @pl.when(has_cross)
@@ -478,11 +482,18 @@
 
             pl.when(r == 0)(ghost_setup)
 
-            extra = jnp.zeros_like(force)
+            extra = ghost_extra = jnp.zeros_like(force)
             if site:
                 for m in range(3):
                     layer_copy(n, m).wait_recv()
+
+                @pl.when(has_cross)
+                def _():
+                    for m in range(3):
+                        layer_ghost(r, m).wait_recv()
+
                 extra = layer_terms(own, v, b["layer_recv"], n)
+                ghost_extra = layer_terms(ghost, gv, b["layer_far"], r)
 
             @pl.when(has_mate)
             def _():
@@ -512,15 +523,7 @@
             def _():
                 mate_copy(n + 1).start()
 
-            extra = jnp.zeros_like(force)
-            if site:
-
-                @pl.when(has_cross)
-                def _():
-                    for m in range(3):
-                        layer_ghost(r, m).wait_recv()
-
-                extra = layer_terms(ghost, gv, b["layer_far"], r)
+            extra = ghost_extra
 
             @pl.when(has_beyond)
             def _():
@@ -555,8 +558,16 @@
             own["u"][...] = later
             if not site:
                 send_layer(n + 1, later)
+
+            @pl.when(r < ROUNDS - 1)
+            def _():
+                own["force"][...] = element_forces(d, own)
+
             return carry
 
+        own["force"][...] = element_forces(d, own)
+        if not site:
+            meet_and_share()
         lax.fori_loop(0, ROUNDS, body, 0)
         out = site_out if site else reg_out
         for c in range(3):
@@ -607,6 +618,16 @@
     def _():
         reg_out[...] = jnp.zeros_like(reg_out)
         role(True)
+
+
+def write_out(reg_in, site_in, reg_out, site_out, sem):
+    copies = [
+        pltpu.make_async_copy(src, dst, sem.at[k]) for k, (src, dst) in enumerate(((site_in, site_out), (reg_in, reg_out)))
+    ]
+    for copy in copies:
+        copy.start()
+    for copy in copies:
+        copy.wait()
 
 
 def solution(mesh):
@@ -681,7 +702,16 @@
                 collective_id=0, has_side_effects=True, vmem_limit_bytes=32 * 1024 * 1024
             ),
         )(*[arg if k == SCALAR else pltpu.with_memory_space_constraint(arg, pltpu.HBM) for k, arg in enumerate(args)])
-        return tuple(out.reshape(1, 1, out.shape[0], out.shape[2]) for out in (reg_out, site_out))
+        outs = (reg_out, site_out)
+        outs = pl.pallas_call(
+            write_out,
+            out_shape=tuple(jax.ShapeDtypeStruct(out.shape, F32) for out in outs),
+            in_specs=[vmem] * 2,
+            out_specs=(hbm, hbm),
+            scratch_shapes=[dma((2,))],
+            compiler_params=pltpu.CompilerParams(vmem_limit_bytes=1024 * 1024),
+        )(*outs)
+        return tuple(out.reshape(1, 1, out.shape[0], out.shape[2]) for out in outs)
 
     cell = ("grp", "sub")
     specs = [P(*cell)] * 21

time: 32.5 us -> 31.6 us (0.972)
  local copies, waits for them, and re-layouts: 1.2 us -> 0 us
  Pallas kernels: 29.7 us -> 30.1 us
    unnamed x2 -> x0, local copies, waits for them, and re-layouts: 1.2 us -> none
    pallas_call x0 -> x1, Pallas kernels: none -> 0.63 us  [shards(): pl.pallas_call(write_out, out_shape=tuple((jax.ShapeDtypeStruct(out.shape...]
where the time goes in v3:
time: 31.6 us; the launch traced here: 31.4 us
  Pallas kernels  30.1 us (95%)
  between operations  1.29 us (4%)
    pallas_call x1, Pallas kernels, shards(): pl.pallas_call(functools.partial(kernel, n_grp, n_sub, rd, sd, slots, key...  29.5 us

profile of v3, /device:TPU:7, one launch (start us, length us, event | category | flops | bytes accessed | tf_op | source)
XLA Modules:
  0.0 31.4 jit_solution(17768452720133889314)
XLA Ops:
  1.3 29.5 %shard_map.212 = (f32[3,1,384]{2,1,0:T(1,128)S(1)}, f32[3,1,1536]{2,1,0:T(1,128)S(1)}) custom-call(f32[3,1,384]{2,1,0:T(1,128)} %bitcast.28, f32[3,1,384]{2,1,0:T(1,128)} %bitcast.29, f32[3,1,1536]{2,1,0:T(1,128)} %bitcast.24, f32[3,1,1536]{2,1,0:T(1,128)} %bitcast.25, s32[10,1,256]{2,1,0:T(1,128)} %bitcast.27, s32[35,1,128]{2,1,0:T(1,128)} %bitcast.26, ...), custom_call_target="tpu_custom_call" | custom-call | tf_op jit(solution)/shard_map/pallas_call | solution.py:692
  30.8 0.6 %shard_map.213 = (f32[3,1,384]{2,1,0:T(1,128)}, f32[3,1,1536]{2,1,0:T(1,128)}) custom-call(f32[3,1,384]{2,1,0:T(1,128)S(1)} %get-tuple-element.6.reg_in, f32[3,1,1536]{2,1,0:T(1,128)S(1)} %get-tuple-element.7.site_in), custom_call_target="tpu_custom_call" | custom-call | tf_op jit(solution)/shard_map/pallas_call | solution.py:706

commit v4 on v3

--- a/solution.py
+++ b/solution.py
@@ -54,13 +54,13 @@
     h = -(-count // width)
     qp = up(q, 8)
     return dict(
-        p=p, e=e, q=q, count=count, width=width, shift=width.bit_length() - 1, h=h, hp=up(h, 8), qp=qp,
+        p=p, e=e, q=q, count=count, width=width, shift=width.bit_length() - 1, h=h, hp=h, rows=up(3 * h, 8), qp=qp,
         p8=up(p, 8), kw=up(9 * qp, LANES),
     )
 
 
 def part_scratch(d, slot_rows, slots):
-    state = (3 * d["hp"], d["width"])
+    state = (d["rows"], d["width"])
     return dict(
         lane=pltpu.VMEM((d["p8"], d["e"]), jnp.int32),
         block=pltpu.VMEM((d["p8"], d["e"]), jnp.int32),
@@ -75,7 +75,7 @@
 
 
 def role_scratch(d, slots):
-    state = (3 * d["hp"], d["width"])
+    state = (d["rows"], d["width"])
     return dict(
         wide=pltpu.VMEM((2, d["p8"], d["kw"]), F32),
         weight=pltpu.VMEM((2, up(d["p"] * d["p8"], 16), d["kw"]), BF16),
@@ -161,9 +161,23 @@
 
 
 def spread(d, rows, blocks):
-    lanes = rows[0].shape[1]
-    mine = lax.broadcasted_iota(jnp.int32, (d["hp"], lanes), 0) == blocks
-    return jnp.concatenate([jnp.where(mine, row, 0.0) for row in rows], axis=0).astype(BF16)
+    lanes, hp = rows[0].shape[1], d["hp"]
+    place = lax.broadcasted_iota(jnp.int32, (8, lanes), 0)
+    out = []
+    for k in range(len(rows) // 3):
+        for first in range(0, d["rows"], 8):
+            value, wanted = None, None
+            for c in range(3):
+                low, high = c * hp - first, (c + 1) * hp - first
+                if high <= 0 or low >= 8:
+                    continue
+                row, block = jnp.broadcast_to(rows[3 * k + c], (8, lanes)), place - low
+                value = row if value is None else jnp.where(place < low, value, row)
+                wanted = block if wanted is None else jnp.where(place < low, wanted, block)
+            if first + 8 > 3 * hp:
+                wanted = jnp.where(place < 3 * hp - first, wanted, -2)
+            out.append(jnp.where(wanted == blocks, value, 0.0))
+    return jnp.concatenate(out, axis=0).astype(BF16)
 
 
 def spread_block(d, block, index):
@@ -174,25 +188,18 @@
 
 
 def join(d, total):
-    half = 3 * d["hp"]
+    half = d["rows"]
     return total[0:half] + total[half:]
 
 
 def pick(d, field, index, live):
-    hp, slots = d["hp"], index.shape[1]
-    lane = jnp.broadcast_to(index & (LANES - 1), (hp, slots))
-    blocks = jnp.where(live, index >> d["shift"], -1)
-    mine = lax.broadcasted_iota(jnp.int32, (hp, slots), 0) == blocks
-    parts = d["width"] // LANES
-    which = jnp.broadcast_to((index >> 7) & (parts - 1), (hp, slots))
-    out = []
-    for c in range(3):
-        rows = field[c * hp : (c + 1) * hp]
-        got = lane_gather(rows[:, 0:LANES], lane)
-        for k in range(1, parts):
-            got = jnp.where(which == k, lane_gather(rows[:, k * LANES : (k + 1) * LANES], lane), got)
-        out.append(jnp.sum(jnp.where(mine, got, 0.0), axis=0, keepdims=True))
-    return out
+    count, slots = d["rows"], index.shape[1]
+    got = lane_gather(field, jnp.broadcast_to(index & (LANES - 1), (count, slots)))
+    blocks = jnp.where(live, index >> d["shift"], -4 * count)
+    place = lax.broadcasted_iota(jnp.int32, (count, slots), 0)
+    return [
+        jnp.sum(jnp.where(place == blocks + c * d["hp"], got, 0.0), axis=0, keepdims=True) for c in range(3)
+    ]
 
 
 def element_forces(d, s):

time: 31.6 us -> 31.1 us (0.984)
  Pallas kernels: 30.1 us -> 29.6 us
    pallas_call x1, Pallas kernels: 29.5 us -> 29 us  [shards(): pl.pallas_call(functools.partial(kernel, n_grp, n_sub, rd, sd, slots, key...]
where the time goes in v4:
time: 31.1 us; the launch traced here: 30.9 us
  Pallas kernels  29.6 us (95%)
  between operations  1.29 us (4%)
    pallas_call x1, Pallas kernels, shards(): pl.pallas_call(functools.partial(kernel, n_grp, n_sub, rd, sd, slots, key...  29 us
    pallas_call x1, Pallas kernels, shards(): pl.pallas_call(write_out, out_shape=tuple((jax.ShapeDtypeStruct(out.shape...  0.63 us

profile of v4, /device:TPU:7, one launch (start us, length us, event | category | flops | bytes accessed | tf_op | source)
XLA Modules:
  0.0 30.9 jit_solution(11670744203418594704)
XLA Ops:
  1.3 29.0 %shard_map.212 = (f32[3,1,384]{2,1,0:T(1,128)S(1)}, f32[3,1,1536]{2,1,0:T(1,128)S(1)}) custom-call(f32[3,1,384]{2,1,0:T(1,128)} %bitcast.28, f32[3,1,384]{2,1,0:T(1,128)} %bitcast.29, f32[3,1,1536]{2,1,0:T(1,128)} %bitcast.24, f32[3,1,1536]{2,1,0:T(1,128)} %bitcast.25, s32[10,1,256]{2,1,0:T(1,128)} %bitcast.27, s32[35,1,128]{2,1,0:T(1,128)} %bitcast.26, ...), custom_call_target="tpu_custom_call" | custom-call | tf_op jit(solution)/shard_map/pallas_call | solution.py:699
  30.3 0.6 %shard_map.213 = (f32[3,1,384]{2,1,0:T(1,128)}, f32[3,1,1536]{2,1,0:T(1,128)}) custom-call(f32[3,1,384]{2,1,0:T(1,128)S(1)} %get-tuple-element.6.reg_in, f32[3,1,1536]{2,1,0:T(1,128)S(1)} %get-tuple-element.7.site_in), custom_call_target="tpu_custom_call" | custom-call | tf_op jit(solution)/shard_map/pallas_call | solution.py:713

commit v5 on v4

--- a/solution.py
+++ b/solution.py
@@ -92,11 +92,12 @@
     length = rows[0].shape[1]
     for r, row in enumerate(rows):
         turn[r : r + 1, 0:length] = (row & (d["width"] - 1)).astype(F32)
-    columns = turn[:, 0:length].T
-    lane = lax.broadcasted_iota(jnp.int32, (length, d["width"]), 1).astype(F32)
+    columns = turn[:, 0:length].T.astype(BF16)
+    lane = lax.broadcasted_iota(jnp.int32, (length, d["width"]), 1).astype(F32).astype(BF16)
+    one, zero = jnp.ones((), BF16), jnp.zeros((), BF16)
     for r in range(len(rows)):
-        hot = jnp.where(lane == columns[:, r : r + 1], 1.0, 0.0)
-        out_ref[r * length : (r + 1) * length, :] = hot.astype(BF16)
+        hot = jnp.where(lane == columns[:, r : r + 1], one, zero)
+        out_ref[r * length : (r + 1) * length, :] = hot
 
 
 def fill_tables(d, s, table, square):

time: 31.1 us -> 30.9 us (level)
  no operation moved by 1% of the time
where the time goes in v5:
time: 30.9 us; the launch traced here: 30.7 us
  Pallas kernels  29.4 us (95%)
  between operations  1.29 us (4%)
    pallas_call x1, Pallas kernels, shards(): pl.pallas_call(functools.partial(kernel, n_grp, n_sub, rd, sd, slots, key...  28.8 us
    pallas_call x1, Pallas kernels, shards(): pl.pallas_call(write_out, out_shape=tuple((jax.ShapeDtypeStruct(out.shape...  0.63 us

profile of v5, /device:TPU:7, one launch (start us, length us, event | category | flops | bytes accessed | tf_op | source)
XLA Modules:
  0.0 30.7 jit_solution(11746904635728901678)
XLA Ops:
  1.3 28.8 %shard_map.212 = (f32[3,1,384]{2,1,0:T(1,128)S(1)}, f32[3,1,1536]{2,1,0:T(1,128)S(1)}) custom-call(f32[3,1,384]{2,1,0:T(1,128)} %bitcast.28, f32[3,1,384]{2,1,0:T(1,128)} %bitcast.29, f32[3,1,1536]{2,1,0:T(1,128)} %bitcast.24, f32[3,1,1536]{2,1,0:T(1,128)} %bitcast.25, s32[10,1,256]{2,1,0:T(1,128)} %bitcast.27, s32[35,1,128]{2,1,0:T(1,128)} %bitcast.26, ...), custom_call_target="tpu_custom_call" | custom-call | tf_op jit(solution)/shard_map/pallas_call | solution.py:700
  30.1 0.6 %shard_map.213 = (f32[3,1,384]{2,1,0:T(1,128)}, f32[3,1,1536]{2,1,0:T(1,128)}) custom-call(f32[3,1,384]{2,1,0:T(1,128)S(1)} %get-tuple-element.6.reg_in, f32[3,1,1536]{2,1,0:T(1,128)S(1)} %get-tuple-element.7.site_in), custom_call_target="tpu_custom_call" | custom-call | tf_op jit(solution)/shard_map/pallas_call | solution.py:714
